TPU v7x, 32 devices: a whole 2x2x4 slice. The times are simulated.
32 devices in a mesh: ty: 4 (over y, x), tx: 8 (over z, core).
Axes of the slice: x: 2, y: 2, z: 4, core: 2. Of those that a mesh axis runs over, the one named last changes fastest.
Arguments:
- object_slices: float32 [2, 2, 1024, 2048], P(None, None, 'ty', 'tx'), may hold values from -5 to 5
- probe: float32 [2, 256, 256], replicated, may hold values from -5 to 5
- position_count: int32 [4, 8], P('ty', 'tx'), may hold values from 1 to 5, as said below
- offsets: int32 [4, 8, 5, 2], P('ty', 'tx'), may hold values from 0 to 128
- intensities: float32 [4, 8, 5, 256, 256], P('ty', 'tx'), may hold values from 0 to 2
Outputs:
- object_new: float32 [2, 2, 1024, 2048], P(None, None, 'ty', 'tx')
- probe_new: float32 [2, 256, 256], replicated
Inputs may be any that keep to these rules, and one draw needn't show every extreme that they name: `position_count`: each tile has 1 to 5 positions; some tile has exactly 5.
All inputs are finite; a program needn't handle non-finite values.
Results may differ from a plain program's by a relative error of at most 0.0003.
Values sent between devices are 32-bit elements; how exact they have to be, the bound alone decides.
No kernel may reach another device: no remote copies, remote signals or barrier semaphores. Data moves between devices by JAX's collectives and lax.ppermute only.
A program may use at most 128 MiB of HBM per device.

v0:
```python
import math
import jax
import jax.numpy as jnp
from jax import lax
from jax.sharding import PartitionSpec as P

PROBE = 256
CORE = 256
MARGIN = 64
ITERS = 2
chirp_rate = 0.5
object_rate = 0.5
probe_rate = 2.0


def extended_2(block, sides, width):
    for axis, dim in sides:
        count = lax.axis_size(axis)
        forward = [(i, i + 1) for i in range(count - 1)]
        forward.append((count - 1, 0))
        backward = [(target, source) for source, target in forward]
        low = lax.ppermute(
            lax.slice_in_dim(block, block.shape[dim] - width, None, axis=dim), axis, forward
        )
        high = lax.ppermute(lax.slice_in_dim(block, 0, width, axis=dim), axis, backward)
        block = jnp.concatenate([low, block, high], axis=dim)
    return block


def matmul(left, right):
    return jnp.dot(left, right, precision=lax.Precision.HIGHEST, preferred_element_type=jnp.float32)


def complex_product(left_real, left_imag, right_real, right_imag):
    out_real = matmul(left_real, right_real) - matmul(left_imag, right_imag)
    out_imag = matmul(left_real, right_imag) + matmul(left_imag, right_real)
    return (out_real, out_imag)


def dft_tables(size):
    index = lax.iota(jnp.int32, size)
    product = index[:, None] * index[None, :] % size
    angles = product.astype(jnp.float32) * (2.0 * math.pi / size)
    factor = 1.0 / math.sqrt(size)
    four_real = jnp.cos(angles) * factor
    four_imag = -jnp.sin(angles) * factor
    centred = ((index + size // 2) % size - size // 2).astype(jnp.float32)
    phases = centred * centred * (chirp_rate * math.pi / size)
    kernel_real = jnp.cos(phases)
    kernel_imag = -jnp.sin(phases)
    scaled_real = four_real * kernel_real[None, :] + four_imag * kernel_imag[None, :]
    scaled_imag = four_real * kernel_imag[None, :] - four_imag * kernel_real[None, :]
    prop_real, prop_imag = complex_product(scaled_real, scaled_imag, four_real, four_imag)
    return (four_real, four_imag, prop_real, prop_imag)


def forward_pair(mat_real, mat_imag, field_real, field_imag):
    mid_real, mid_imag = complex_product(mat_real, mat_imag, field_real, field_imag)
    return complex_product(mid_real, mid_imag, mat_real.T, mat_imag.T)


def adjoint_pair(mat_real, mat_imag, field_real, field_imag):
    mid_real, mid_imag = complex_product(mat_real.T, -mat_imag.T, field_real, field_imag)
    return complex_product(mid_real, mid_imag, mat_real, -mat_imag)


def position_grad(probe_now, window, measured, tables):
    four_real, four_imag, prop_real, prop_imag = tables
    probe_real, probe_imag = (probe_now[0], probe_now[1])
    one_real, one_imag, two_real, two_imag = (window[0], window[1], window[2], window[3])
    wave_real = probe_real * one_real - probe_imag * one_imag
    wave_imag = probe_real * one_imag + probe_imag * one_real
    moved_real, moved_imag = forward_pair(prop_real, prop_imag, wave_real, wave_imag)
    exit_real = moved_real * two_real - moved_imag * two_imag
    exit_imag = moved_real * two_imag + moved_imag * two_real
    far_real, far_imag = forward_pair(four_real, four_imag, exit_real, exit_imag)
    misfit = far_real * far_real + far_imag * far_imag - measured
    back_real, back_imag = adjoint_pair(four_real, four_imag, misfit * far_real, misfit * far_imag)
    grad_two_real = moved_real * back_real + moved_imag * back_imag
    grad_two_imag = moved_real * back_imag - moved_imag * back_real
    gmove_real = two_real * back_real + two_imag * back_imag
    gmove_imag = two_real * back_imag - two_imag * back_real
    gwave_real, gwave_imag = adjoint_pair(prop_real, prop_imag, gmove_real, gmove_imag)
    grad_one_real = probe_real * gwave_real + probe_imag * gwave_imag
    grad_one_imag = probe_real * gwave_imag - probe_imag * gwave_real
    gprobe_real = one_real * gwave_real + one_imag * gwave_imag
    gprobe_imag = one_real * gwave_imag - one_imag * gwave_real
    object_part = jnp.stack([grad_one_real, grad_one_imag, grad_two_real, grad_two_imag])
    return (object_part, jnp.stack([gprobe_real, gprobe_imag]))


def fold_axis(padded, width, dim):
    extent = padded.shape[dim] - 2 * width
    middle = lax.slice_in_dim(padded, width, width + extent, axis=dim)
    before = lax.slice_in_dim(padded, 0, width, axis=dim)
    after = lax.slice_in_dim(padded, width + extent, extent + 2 * width, axis=dim)
    spec_before = [(0, 0)] * padded.ndim
    spec_before[dim] = (2 * MARGIN - width, extent - 2 * MARGIN)
    spec_after = [(0, 0)] * padded.ndim
    spec_after[dim] = (CORE, extent - CORE - width)
    return middle + jnp.pad(before, spec_before) + jnp.pad(after, spec_after)


def fold_sums(padded, width):
    return fold_axis(fold_axis(padded, width, 1), width, 2)


def body(object_slices, probe, position_count, offsets, intensities):
    tables = dft_tables(PROBE)
    extent = CORE + 2 * MARGIN
    zero = jnp.int32(0)
    count = position_count[0, 0]
    core = object_slices.reshape(4, CORE, CORE)
    extended = extended_2(core, (("ty", 1), ("tx", 2)), MARGIN)
    probe_now = probe
    devices = lax.axis_size("ty") * lax.axis_size("tx")
    for step in range(ITERS):

        def visit(slot, carry):
            local, local_probe = carry
            top = offsets[0, 0, slot, 0]
            left = offsets[0, 0, slot, 1]
            window = lax.dynamic_slice(extended, (zero, top, left), (4, PROBE, PROBE))
            object_part, probe_part = position_grad(
                probe_now, window, intensities[0, 0, slot], tables
            )
            current = lax.dynamic_slice(local, (zero, top, left), (4, PROBE, PROBE))
            local = lax.dynamic_update_slice(local, current + object_part, (zero, top, left))
            return (local, local_probe + probe_part)

        start = (
            jnp.zeros((4, extent, extent), jnp.float32),
            jnp.zeros((2, PROBE, PROBE), jnp.float32),
        )
        grads, probe_grad = lax.fori_loop(zero, count, visit, start)
        peak = jnp.max(probe_now[0] * probe_now[0] + probe_now[1] * probe_now[1]) + 1e-06
        padded = extended_2(grads, (("ty", 1), ("tx", 2)), MARGIN)
        total = fold_sums(padded, MARGIN)[:, MARGIN : MARGIN + CORE, MARGIN : MARGIN + CORE]
        core = core - object_rate / peak * total
        if step + 1 < ITERS:
            extended = extended_2(core, (("ty", 1), ("tx", 2)), MARGIN)
        summed = lax.psum(probe_grad, ("ty", "tx"))
        probe_now = probe_now - probe_rate / devices * summed
    return (core.reshape(2, 2, CORE, CORE), probe_now)


def solution(mesh):
    placed = (
        P(None, None, "ty", "tx"),
        P(),
        P("ty", "tx"),
        P("ty", "tx", None, None),
        P("ty", "tx", None, None, None),
    )
    return jax.shard_map(
        body,
        mesh=mesh,
        in_specs=placed,
        out_specs=(P(None, None, "ty", "tx"), P()),
        check_vma=False,
    )
```

profile of v0, /device:TPU:0, one launch (start us, length us, event | category | flops | bytes accessed | tf_op | source)
XLA Modules:
  0.0 1035.9 jit_solution(13837448059332774943)
XLA Ops:
  17.1 9.8 collective-permute-done
  26.9 10.6 %collective-permute-done.1 = f32[4,64,256]{1,2,0:T(8,128)S(1)} collective-permute-done((f32[4,64,256]{1,2,0:T(8,128)}, f32[4,64,256]{1,2,0:T(8,128)S(1)}, u32[]{:S(2)}, u32[]{:S(2)}) %collective-permute-start.1) | collective-permute-done | bytes 262176 | tf_op jit(solution)/shard_map/ppermute | solution.py:25
  38.0 3.5 collective-permute-start.3
  44.5 4.6 collective-permute-done.2
  54.6 203.5 %while.32 = (s32[]{:T(128)}, f32[4,384,384]{2,1,0:T(8,128)}, f32[2,256,256]{2,1,0:T(8,128)}, s32[]{:T(128)}, s32[1,1,5,2]{2,3,1,0:T(2,128)S(1)}, /*index=5*/f32[...) while((s32[]{:T(128)}, f32[4,384,384]{2,1,0:T(8,128)}, ...), condition=%wide.region_2.3_spmd.clone.clone, body=%wide.region_1.2_spmd.clone.clone.sunk | while | flops 6464077824 | bytes 48234916 | solution.py:135
  125.1 11.5 %dynamic_update_slice.16 = f32[4,384,384]{2,1,0:T(8,128)} dynamic-update-slice(f32[4,384,384]{2,1,0:T(8,128)} %get-tuple-element.1014, f32[4,256,256]{2,1,0:T(8,128)S(1)} %maximum_add_fusion.8, s32[]{:T(128)} %constant.70.clone.1..sunk, s32[]{:T(128)S(6)} %select_n.366, s32[]{:T(128)S(6)} %select_n.367) | dynamic-update-slice | bytes 2097156 | tf_op jit(solution)/shard_map/while/body/dynamic_update_slice | solution.py:128
  183.1 11.3 %dynamic_update_slice.16 = f32[4,384,384]{2,1,0:T(8,128)} dynamic-update-slice(f32[4,384,384]{2,1,0:T(8,128)} %get-tuple-element.1014, f32[4,256,256]{2,1,0:T(8,128)S(1)} %maximum_add_fusion.8, s32[]{:T(128)} %constant.70.clone.1..sunk, s32[]{:T(128)S(6)} %select_n.366, s32[]{:T(128)S(6)} %select_n.367) | dynamic-update-slice | bytes 2097156 | tf_op jit(solution)/shard_map/while/body/dynamic_update_slice | solution.py:128
  240.9 11.5 %dynamic_update_slice.16 = f32[4,384,384]{2,1,0:T(8,128)} dynamic-update-slice(f32[4,384,384]{2,1,0:T(8,128)} %get-tuple-element.1014, f32[4,256,256]{2,1,0:T(8,128)S(1)} %maximum_add_fusion.8, s32[]{:T(128)} %constant.70.clone.1..sunk, s32[]{:T(128)S(6)} %select_n.366, s32[]{:T(128)S(6)} %select_n.367) | dynamic-update-slice | bytes 2097156 | tf_op jit(solution)/shard_map/while/body/dynamic_update_slice | solution.py:128
  259.3 117.1 %collective-permute-start.5 = (f32[4,64,384]{2,1,0:T(8,128)S(1)}, f32[4,64,384]{2,1,0:T(8,128)S(1)}, u32[]{:S(2)}, u32[]{:S(2)}) collective-permute-start(f32[4,64,384]{2,1,0:T(8,128)S(1)} %get-tuple-element.749), channel_id=1, source_target_pairs={{8,0},{16,8},{24,16},{0,24},{9,1},{17,9},{25,17},{1,25},{10,2},{18... | collective-permute-start | bytes 1179656 | tf_op jit(solution)/shard_map/ppermute | solution.py:25
  379.5 4.3 collective-permute-done.4
  388.7 4.3 collective-permute-start.6
  394.3 7.8 collective-permute-done.6
  413.8 8.9 collective-permute-start.8
  422.7 13.3 %collective-permute-done.8 = f32[4,64,256]{1,2,0:T(8,128)S(1)} collective-permute-done((f32[4,64,256]{1,2,0:T(8,128)}, f32[4,64,256]{1,2,0:T(8,128)S(1)}, u32[]{:S(2)}, u32[]{:S(2)}) %collective-permute-start.8) | collective-permute-done | bytes 262176 | tf_op jit(solution)/shard_map/ppermute | solution.py:22
  436.0 11.2 %collective-permute-done.9 = f32[4,64,256]{1,2,0:T(8,128)} collective-permute-done((f32[4,64,256]{1,2,0:T(8,128)}, f32[4,64,256]{1,2,0:T(8,128)}, u32[]{:S(2)}, u32[]{:S(2)}) %collective-permute-start.9) | collective-permute-done | bytes 262176 | tf_op jit(solution)/shard_map/ppermute | solution.py:25
  449.4 3.5 collective-permute-start.11
  452.9 100.7 %all-reduce.11.cloned.1.call-done = f32[2,256,256]{2,1,0:T(8,128)} async-done(((f32[2,256,256]{2,1,0:T(8,128)}), f32[2,256,256]{2,1,0:T(8,128)}) %all-reduce.11.cloned.1.call-update) | async-done | bytes 524304 | tf_op jit(solution)/shard_map/psum | solution.py:142
  560.5 204.1 %while.33 = (s32[]{:T(128)}, f32[4,384,384]{2,1,0:T(8,128)}, f32[2,256,256]{2,1,0:T(8,128)}, s32[]{:T(128)}, s32[1,1,5,2]{2,3,1,0:T(2,128)S(1)}, /*index=5*/f32[...) while((s32[]{:T(128)}, f32[4,384,384]{2,1,0:T(8,128)}, ...), condition=%wide.region_6.7_spmd.clone.clone, body=%wide.region_5.6_spmd.clone.clone.sunk | while | flops 6464077824 | bytes 48234916 | solution.py:135
  631.4 11.5 %dynamic_update_slice.17 = f32[4,384,384]{2,1,0:T(8,128)} dynamic-update-slice(f32[4,384,384]{2,1,0:T(8,128)} %get-tuple-element.1071, f32[4,256,256]{2,1,0:T(8,128)S(1)} %maximum_add_fusion.10, s32[]{:T(128)} %constant.70.clone.1..sunk.1, s32[]{:T(128)S(6)} %select_n.385, s32[]{:T(128)S(6)} %select_n.386) | dynamic-update-slice | bytes 2097156 | tf_op jit(solution)/shard_map/while/body/dynamic_update_slice | solution.py:128
  690.0 11.3 %dynamic_update_slice.17 = f32[4,384,384]{2,1,0:T(8,128)} dynamic-update-slice(f32[4,384,384]{2,1,0:T(8,128)} %get-tuple-element.1071, f32[4,256,256]{2,1,0:T(8,128)S(1)} %maximum_add_fusion.10, s32[]{:T(128)} %constant.70.clone.1..sunk.1, s32[]{:T(128)S(6)} %select_n.385, s32[]{:T(128)S(6)} %select_n.386) | dynamic-update-slice | bytes 2097156 | tf_op jit(solution)/shard_map/while/body/dynamic_update_slice | solution.py:128
  748.5 11.5 %dynamic_update_slice.17 = f32[4,384,384]{2,1,0:T(8,128)} dynamic-update-slice(f32[4,384,384]{2,1,0:T(8,128)} %get-tuple-element.1071, f32[4,256,256]{2,1,0:T(8,128)S(1)} %maximum_add_fusion.10, s32[]{:T(128)} %constant.70.clone.1..sunk.1, s32[]{:T(128)S(6)} %select_n.385, s32[]{:T(128)S(6)} %select_n.386) | dynamic-update-slice | bytes 2097156 | tf_op jit(solution)/shard_map/while/body/dynamic_update_slice | solution.py:128
  765.8 119.2 %collective-permute-start.13 = (f32[4,64,384]{2,1,0:T(8,128)S(1)}, f32[4,64,384]{2,1,0:T(8,128)S(1)}, u32[]{:S(2)}, u32[]{:S(2)}) collective-permute-start(f32[4,64,384]{2,1,0:T(8,128)S(1)} %get-tuple-element.747), channel_id=1, source_target_pairs={{8,0},{16,8},{24,16},{0,24},{9,1},{17,9},{25,17},{1,25},{10,2},{18... | collective-permute-start | bytes 1179656 | tf_op jit(solution)/shard_map/ppermute | solution.py:25
  888.1 6.8 collective-permute-done.12
  902.9 116.5 %all-reduce.13.cloned.1.call-done = f32[2,256,256]{2,1,0:T(8,128)} async-done(((f32[2,256,256]{2,1,0:T(8,128)}), f32[2,256,256]{2,1,0:T(8,128)}) %all-reduce.13.cloned.1.call-update) | async-done | bytes 524304 | tf_op jit(solution)/shard_map/psum | solution.py:142
  (355 shorter events, 324.2 us)
Async XLA Ops:
  7.2 546.4 %all-reduce.11.cloned.1.call-start = ((), (), s32[]{:S(2)}) async-start(), calls=%async_computation | async-start | bytes 1048576 | tf_op jit(solution)/shard_map/psum | solution.py:142
  8.8 40.3 %copy-start.3 = (f32[2,2,256,256]{2,3,1,0:T(8,128)}, f32[2,2,256,256]{2,3,1,0:T(8,128)S(1)}, u32[]{:S(2)}) copy-start(f32[2,2,256,256]{2,3,1,0:T(8,128)S(1)} %copy.21) | copy-start | bytes 3145732
  10.0 16.9 %collective-permute-start = (f32[4,64,256]{1,2,0:T(8,128)}, f32[4,64,256]{1,2,0:T(8,128)S(1)}, u32[]{:S(2)}, u32[]{:S(2)}) collective-permute-start(f32[4,64,256]{1,2,0:T(8,128)} %get-tuple-element.756), channel_id=1, source_target_pairs={{0,8},{8,16},{16,24},{24,0},{1,9},{9,17},{17,25},{25,1},{2,10},{10... | collective-permute-start | bytes 786440 | tf_op jit(solution)/shard_map/ppermute | solution.py:22
  13.0 24.6 %collective-permute-start.1 = (f32[4,64,256]{1,2,0:T(8,128)}, f32[4,64,256]{1,2,0:T(8,128)S(1)}, u32[]{:S(2)}, u32[]{:S(2)}) collective-permute-start(f32[4,64,256]{1,2,0:T(8,128)} %get-tuple-element.757), channel_id=1, source_target_pairs={{8,0},{16,8},{24,16},{0,24},{9,1},{17,9},{25,17},{1,25},{10,2},{18... | collective-permute-start | bytes 786440 | tf_op jit(solution)/shard_map/ppermute | solution.py:25
  37.9 11.2 %collective-permute-start.2 = (f32[4,384,64]{1,2,0:T(8,128)S(1)}, f32[4,384,64]{1,2,0:T(8,128)S(1)}, u32[]{:S(2)}, u32[]{:S(2)}) collective-permute-start(f32[4,384,64]{1,2,0:T(8,128)S(1)} %get-tuple-element.752), channel_id=1, source_target_pairs={{0,1},{1,2},{2,3},{3,4},{4,5},{5,6},{6,7},{7,0},{8,9},{9,10},{10,1... | collective-permute-start | bytes 1179656 | tf_op jit(solution)/shard_map/ppermute | solution.py:22
  38.0 11.1 %collective-permute-start.3 = (f32[4,384,64]{1,2,0:T(8,128)S(1)}, f32[4,384,64]{1,2,0:T(8,128)S(1)}, u32[]{:S(2)}, u32[]{:S(2)}) collective-permute-start(f32[4,384,64]{1,2,0:T(8,128)S(1)} %get-tuple-element.753), channel_id=1, source_target_pairs={{1,0},{2,1},{3,2},{4,3},{5,4},{6,5},{7,6},{0,7},{9,8},{10,9},{11,1... | collective-permute-start | bytes 1179656 | tf_op jit(solution)/shard_map/ppermute | solution.py:25
  123.1 13.5 %copy-start.10 = (f32[2,256,256]{2,1,0:T(8,128)}, f32[2,256,256]{2,1,0:T(8,128)S(1)}, u32[]{:S(2)}) copy-start(f32[2,256,256]{2,1,0:T(8,128)S(1)} %maximum_add_fusion.9) | copy-start | bytes 1572868 | tf_op jit(solution)/shard_map/while
  238.9 13.5 %copy-start.10 = (f32[2,256,256]{2,1,0:T(8,128)}, f32[2,256,256]{2,1,0:T(8,128)S(1)}, u32[]{:S(2)}) copy-start(f32[2,256,256]{2,1,0:T(8,128)S(1)} %maximum_add_fusion.9) | copy-start | bytes 1572868 | tf_op jit(solution)/shard_map/while
  259.3 124.5 %collective-permute-start.4 = (f32[4,64,384]{2,1,0:T(8,128)S(1)}, f32[4,64,384]{2,1,0:T(8,128)}, u32[]{:S(2)}, u32[]{:S(2)}) collective-permute-start(f32[4,64,384]{2,1,0:T(8,128)S(1)} %get-tuple-element.748), channel_id=1, source_target_pairs={{0,8},{8,16},{16,24},{24,0},{1,9},{9,17},{17,25},{25,1},{2,10},{10... | collective-permute-start | bytes 1179656 | tf_op jit(solution)/shard_map/ppermute | solution.py:22
  259.3 126.6 %collective-permute-start.5 = (f32[4,64,384]{2,1,0:T(8,128)S(1)}, f32[4,64,384]{2,1,0:T(8,128)S(1)}, u32[]{:S(2)}, u32[]{:S(2)}) collective-permute-start(f32[4,64,384]{2,1,0:T(8,128)S(1)} %get-tuple-element.749), channel_id=1, source_target_pairs={{8,0},{16,8},{24,16},{0,24},{9,1},{17,9},{25,17},{1,25},{10,2},{18... | collective-permute-start | bytes 1179656 | tf_op jit(solution)/shard_map/ppermute | solution.py:25
  388.7 13.5 %collective-permute-start.6 = (f32[4,512,64]{1,2,0:T(8,128)}, f32[4,512,64]{1,2,0:T(8,128)}, u32[]{:S(2)}, u32[]{:S(2)}) collective-permute-start(f32[4,512,64]{1,2,0:T(8,128)} %get-tuple-element.740), channel_id=1, source_target_pairs={{0,1},{1,2},{2,3},{3,4},{4,5},{5,6},{6,7},{7,0},{8,9},{9,10},{10,1... | collective-permute-start | bytes 1572872 | tf_op jit(solution)/shard_map/ppermute | solution.py:22
  393.0 11.9 %collective-permute-start.7 = (f32[4,512,64]{1,2,0:T(8,128)}, f32[4,512,64]{1,2,0:T(8,128)}, u32[]{:S(2)}, u32[]{:S(2)}) collective-permute-start(f32[4,512,64]{1,2,0:T(8,128)} %get-tuple-element.741), channel_id=1, source_target_pairs={{1,0},{2,1},{3,2},{4,3},{5,4},{6,5},{7,6},{0,7},{9,8},{10,9},{11,1... | collective-permute-start | bytes 1572872 | tf_op jit(solution)/shard_map/ppermute | solution.py:25
  394.3 13.6 %copy-start.2 = (f32[4,384,384]{1,2,0:T(8,128)S(1)}, f32[4,384,384]{1,2,0:T(8,128)}, u32[]{:S(2)}) copy-start(f32[4,384,384]{1,2,0:T(8,128)} %copy.25) | copy-start | bytes 7077892
  412.5 142.2 %copy-start.5 = (f32[4,256,256]{1,2,0:T(8,128)}, f32[4,256,256]{1,2,0:T(8,128)S(1)}, u32[]{:S(2)}) copy-start(f32[4,256,256]{1,2,0:T(8,128)S(1)} %fusion.249) | copy-start | bytes 3145732
  413.8 22.2 %collective-permute-start.8 = (f32[4,64,256]{1,2,0:T(8,128)}, f32[4,64,256]{1,2,0:T(8,128)S(1)}, u32[]{:S(2)}, u32[]{:S(2)}) collective-permute-start(f32[4,64,256]{1,2,0:T(8,128)} %get-tuple-element.754), channel_id=1, source_target_pairs={{0,8},{8,16},{16,24},{24,0},{1,9},{9,17},{17,25},{25,1},{2,10},{10... | collective-permute-start | bytes 786440 | tf_op jit(solution)/shard_map/ppermute | solution.py:22
  422.6 24.5 %collective-permute-start.9 = (f32[4,64,256]{1,2,0:T(8,128)}, f32[4,64,256]{1,2,0:T(8,128)}, u32[]{:S(2)}, u32[]{:S(2)}) collective-permute-start(f32[4,64,256]{1,2,0:T(8,128)} %get-tuple-element.755), channel_id=1, source_target_pairs={{8,0},{16,8},{24,16},{0,24},{9,1},{17,9},{25,17},{1,25},{10,2},{18... | collective-permute-start | bytes 786440 | tf_op jit(solution)/shard_map/ppermute | solution.py:25
  422.7 596.7 %all-reduce.13.cloned.1.call-start = ((), (), s32[]{:S(2)}) async-start(), calls=%async_computation.1 | async-start | bytes 1048576 | tf_op jit(solution)/shard_map/psum | solution.py:142
  436.0 17.0 %copy-start.11 = (f32[4,64,256]{1,2,0:T(8,128)}, f32[4,64,256]{1,2,0:T(8,128)S(1)}, u32[]{:S(2)}) copy-start(f32[4,64,256]{1,2,0:T(8,128)S(1)} %collective-permute-done.8) | copy-start | bytes 786436
  449.4 105.3 %collective-permute-start.10 = (f32[4,384,64]{1,2,0:T(8,128)}, f32[4,384,64]{1,2,0:T(8,128)S(1)}, u32[]{:S(2)}, u32[]{:S(2)}) collective-permute-start(f32[4,384,64]{1,2,0:T(8,128)} %get-tuple-element.750), channel_id=1, source_target_pairs={{0,1},{1,2},{2,3},{3,4},{4,5},{5,6},{6,7},{7,0},{8,9},{9,10},{10,1... | collective-permute-start | bytes 1179656 | tf_op jit(solution)/shard_map/ppermute | solution.py:22
  449.4 105.3 %collective-permute-start.11 = (f32[4,384,64]{1,2,0:T(8,128)}, f32[4,384,64]{1,2,0:T(8,128)}, u32[]{:S(2)}, u32[]{:S(2)}) collective-permute-start(f32[4,384,64]{1,2,0:T(8,128)} %get-tuple-element.751), channel_id=1, source_target_pairs={{1,0},{2,1},{3,2},{4,3},{5,4},{6,5},{7,6},{0,7},{9,8},{10,9},{11,1... | collective-permute-start | bytes 1179656 | tf_op jit(solution)/shard_map/ppermute | solution.py:25
  765.8 129.1 %collective-permute-start.12 = (f32[4,64,384]{2,1,0:T(8,128)S(1)}, f32[4,64,384]{2,1,0:T(8,128)S(1)}, u32[]{:S(2)}, u32[]{:S(2)}) collective-permute-start(f32[4,64,384]{2,1,0:T(8,128)S(1)} %get-tuple-element.746), channel_id=1, source_target_pairs={{0,8},{8,16},{16,24},{24,0},{1,9},{9,17},{17,25},{25,1},{2,10},{10... | collective-permute-start | bytes 1179656 | tf_op jit(solution)/shard_map/ppermute | solution.py:22
  765.8 129.3 %collective-permute-start.13 = (f32[4,64,384]{2,1,0:T(8,128)S(1)}, f32[4,64,384]{2,1,0:T(8,128)S(1)}, u32[]{:S(2)}, u32[]{:S(2)}) collective-permute-start(f32[4,64,384]{2,1,0:T(8,128)S(1)} %get-tuple-element.747), channel_id=1, source_target_pairs={{8,0},{16,8},{24,16},{0,24},{9,1},{17,9},{25,17},{1,25},{10,2},{18... | collective-permute-start | bytes 1179656 | tf_op jit(solution)/shard_map/ppermute | solution.py:25
  898.0 123.3 %collective-permute-start.14 = (f32[4,512,64]{1,2,0:T(8,128)}, f32[4,512,64]{1,2,0:T(8,128)S(1)}, u32[]{:S(2)}, u32[]{:S(2)}) collective-permute-start(f32[4,512,64]{1,2,0:T(8,128)} %get-tuple-element.738), channel_id=1, source_target_pairs={{0,1},{1,2},{2,3},{3,4},{4,5},{5,6},{6,7},{7,0},{8,9},{9,10},{10,1... | collective-permute-start | bytes 1572872 | tf_op jit(solution)/shard_map/ppermute | solution.py:22
  898.1 123.1 %collective-permute-start.15 = (f32[4,512,64]{1,2,0:T(8,128)}, f32[4,512,64]{1,2,0:T(8,128)S(1)}, u32[]{:S(2)}, u32[]{:S(2)}) collective-permute-start(f32[4,512,64]{1,2,0:T(8,128)} %get-tuple-element.739), channel_id=1, source_target_pairs={{1,0},{2,1},{3,2},{4,3},{5,4},{6,5},{7,6},{0,7},{9,8},{10,9},{11,1... | collective-permute-start | bytes 1572872 | tf_op jit(solution)/shard_map/ppermute | solution.py:25
  (16 other events, 65.5 us)
Sparse Core Ops, SparseCore 0:
  422.8 130.7 all-reduce.10
  888.2 131.0 all-reduce.12
where the time goes:
time: 1050 us; the launch traced here: 1040 us
  waiting for transfers between devices  289 us (28%)
  starting transfers between devices  264 us (25%)
  matrix products  211 us (20%)
  local copies, waits for them, and re-layouts  128 us (12%)
  loops' own time  85.2 us (8%)
  other arithmetic  42.3 us (4%)
  between operations  15.9 us (2%)
    ppermute x8, starting transfers between devices, extended_2(): lax.ppermute(lax.slice_in_dim(block, 0, width, axis=dim), axis, backward)  248 us
    psum x2, waiting for transfers between devices, body(): summed = lax.psum(probe_grad, ('ty', 'tx'))  217 us
    dot_general x196, matrix products, matmul(): jnp.dot(left, right, precision=lax.Precision.HIGHEST, preferred_element_t...  211 us
    another operation x2, loops' own time, body(): grads, probe_grad = lax.fori_loop(zero, count, visit, start)  85.2 us
    dynamic_update_slice x6, local copies, waits for them, and re-layouts, visit(): lax.dynamic_update_slice(local, current + object_part, (zero, top, left))  68.5 us
    ppermute x8, waiting for transfers between devices, extended_2(): lax.ppermute(lax.slice_in_dim(block, block.shape[dim] - width, None, axis...  46.6 us
    ppermute x8, waiting for transfers between devices, extended_2(): lax.ppermute(lax.slice_in_dim(block, 0, width, axis=dim), axis, backward)  25.5 us
  transfers between devices with their start and end apart: 18, of which 12 were waited for; matrix products, arithmetic and copies ran while one was open for 2% of the time, Pallas kernels for 0%

commit v1 on v0

--- a/solution.py
+++ b/solution.py
@@ -139,7 +139,7 @@
         core = core - object_rate / peak * total
         if step + 1 < ITERS:
             extended = extended_2(core, (("ty", 1), ("tx", 2)), MARGIN)
-        summed = lax.psum(probe_grad, ("ty", "tx"))
+        summed = jnp.sum(lax.all_gather(probe_grad, ("ty", "tx")), axis=0)
         probe_now = probe_now - probe_rate / devices * summed
     return (core.reshape(2, 2, CORE, CORE), probe_now)
 

time: 1050 us -> 987 us (0.940)
  waiting for transfers between devices: 289 us -> 196 us
  starting transfers between devices: 264 us -> 284 us
    psum x2 -> x0, waiting for transfers between devices: 217 us -> none  [body(): summed = lax.psum(probe_grad, ('ty', 'tx'))]
    all_gather x0 -> x2, waiting for transfers between devices: none -> 86.8 us  [body(): summed = jnp.sum(lax.all_gather(probe_grad, ('ty', 'tx')), axis=0)]
    ppermute x8, starting transfers between devices: 16.4 us -> 41.8 us  [extended_2(): lax.ppermute(lax.slice_in_dim(block, block.shape[dim] - width, None, axis...]
    ppermute x8, waiting for transfers between devices: 25.5 us -> 50.1 us  [extended_2(): lax.ppermute(lax.slice_in_dim(block, 0, width, axis=dim), axis, backward)]
    reduce_sum x0 -> x2, other arithmetic: none -> 13.8 us  [body(): summed = jnp.sum(lax.all_gather(probe_grad, ('ty', 'tx')), axis=0)]
    ppermute x8, waiting for transfers between devices: 46.6 us -> 59 us  [extended_2(): lax.ppermute(lax.slice_in_dim(block, block.shape[dim] - width, None, axis...]
  transfers between devices with their start and end apart: 18 -> 18, of which waited for: 12 -> 16; matrix products, arithmetic and copies ran while one was open for 2% -> 4% of each run, Pallas kernels for 0% -> 0%
where the time goes in v1:
time: 987 us; the launch traced here: 975 us
  starting transfers between devices  284 us (29%)
  matrix products  211 us (21%)
  waiting for transfers between devices  196 us (20%)
  local copies, waits for them, and re-layouts  128 us (13%)
  loops' own time  88.1 us (9%)
  other arithmetic  52.7 us (5%)
  between operations  15.8 us (2%)
    ppermute x8, starting transfers between devices, extended_2(): lax.ppermute(lax.slice_in_dim(block, 0, width, axis=dim), axis, backward)  242 us
    dot_general x196, matrix products, matmul(): jnp.dot(left, right, precision=lax.Precision.HIGHEST, preferred_element_t...  211 us
    another operation x2, loops' own time, body(): grads, probe_grad = lax.fori_loop(zero, count, visit, start)  88.1 us
    all_gather x2, waiting for transfers between devices, body(): summed = jnp.sum(lax.all_gather(probe_grad, ('ty', 'tx')), axis=0)  86.8 us
    dynamic_update_slice x6, local copies, waits for them, and re-layouts, visit(): lax.dynamic_update_slice(local, current + object_part, (zero, top, left))  68.7 us
    ppermute x8, waiting for transfers between devices, extended_2(): lax.ppermute(lax.slice_in_dim(block, block.shape[dim] - width, None, axis...  59 us
    ppermute x8, waiting for transfers between devices, extended_2(): lax.ppermute(lax.slice_in_dim(block, 0, width, axis=dim), axis, backward)  50.1 us
    ppermute x8, starting transfers between devices, extended_2(): lax.ppermute(lax.slice_in_dim(block, block.shape[dim] - width, None, axis...  41.8 us
  transfers between devices with their start and end apart: 18, of which 16 were waited for; matrix products, arithmetic and copies ran while one was open for 4% of the time, Pallas kernels for 0%

profile of v1, /device:TPU:0, one launch (start us, length us, event | category | flops | bytes accessed | tf_op | source)
XLA Modules:
  0.0 975.1 jit_solution(4038876512988222311)
XLA Ops:
  17.2 9.8 %collective-permute-done = f32[4,64,256]{1,2,0:T(8,128)S(1)} collective-permute-done((f32[4,64,256]{1,2,0:T(8,128)}, f32[4,64,256]{1,2,0:T(8,128)S(1)}, u32[]{:S(2)}, u32[]{:S(2)}) %collective-permute-start) | collective-permute-done | bytes 262176 | tf_op jit(solution)/shard_map/ppermute | solution.py:22
  27.0 10.6 %collective-permute-done.1 = f32[4,64,256]{1,2,0:T(8,128)S(1)} collective-permute-done((f32[4,64,256]{1,2,0:T(8,128)}, f32[4,64,256]{1,2,0:T(8,128)S(1)}, u32[]{:S(2)}, u32[]{:S(2)}) %collective-permute-start.1) | collective-permute-done | bytes 262176 | tf_op jit(solution)/shard_map/ppermute | solution.py:25
  54.6 205.7 %while.32 = (s32[]{:T(128)}, f32[4,384,384]{2,1,0:T(8,128)}, f32[2,256,256]{2,1,0:T(8,128)}, s32[]{:T(128)}, s32[1,1,5,2]{2,3,1,0:T(2,128)S(1)}, /*index=5*/f32[...) while((s32[]{:T(128)}, f32[4,384,384]{2,1,0:T(8,128)}, ...), condition=%wide.region_2.3_spmd.clone.clone, body=%wide.region_1.2_spmd.clone.clone.sunk | while | flops 6464077824 | bytes 48234916 | solution.py:135
  125.5 11.5 %dynamic_update_slice.16 = f32[4,384,384]{2,1,0:T(8,128)} dynamic-update-slice(f32[4,384,384]{2,1,0:T(8,128)} %get-tuple-element.1014, f32[4,256,256]{2,1,0:T(8,128)S(1)} %maximum_add_fusion.8, s32[]{:T(128)} %constant.71.clone.1..sunk, s32[]{:T(128)S(6)} %select_n.366, s32[]{:T(128)S(6)} %select_n.367) | dynamic-update-slice | bytes 2097156 | tf_op jit(solution)/shard_map/while/body/dynamic_update_slice | solution.py:128
  184.0 11.3 %dynamic_update_slice.16 = f32[4,384,384]{2,1,0:T(8,128)} dynamic-update-slice(f32[4,384,384]{2,1,0:T(8,128)} %get-tuple-element.1014, f32[4,256,256]{2,1,0:T(8,128)S(1)} %maximum_add_fusion.8, s32[]{:T(128)} %constant.71.clone.1..sunk, s32[]{:T(128)S(6)} %select_n.366, s32[]{:T(128)S(6)} %select_n.367) | dynamic-update-slice | bytes 2097156 | tf_op jit(solution)/shard_map/while/body/dynamic_update_slice | solution.py:128
  242.4 11.5 %dynamic_update_slice.16 = f32[4,384,384]{2,1,0:T(8,128)} dynamic-update-slice(f32[4,384,384]{2,1,0:T(8,128)} %get-tuple-element.1014, f32[4,256,256]{2,1,0:T(8,128)S(1)} %maximum_add_fusion.8, s32[]{:T(128)} %constant.71.clone.1..sunk, s32[]{:T(128)S(6)} %select_n.366, s32[]{:T(128)S(6)} %select_n.367) | dynamic-update-slice | bytes 2097156 | tf_op jit(solution)/shard_map/while/body/dynamic_update_slice | solution.py:128
  261.6 118.0 %collective-permute-start.5 = (f32[4,64,384]{2,1,0:T(8,128)S(1)}, f32[4,64,384]{2,1,0:T(8,128)S(1)}, u32[]{:S(2)}, u32[]{:S(2)}) collective-permute-start(f32[4,64,384]{2,1,0:T(8,128)S(1)} %get-tuple-element.749), channel_id=1, source_target_pairs={{8,0},{16,8},{24,16},{0,24},{9,1},{17,9},{25,17},{1,25},{10,2},{18... | collective-permute-start | bytes 1179656 | tf_op jit(solution)/shard_map/ppermute | solution.py:25
  401.2 13.0 %collective-permute-done.6 = f32[4,512,64]{1,2,0:T(8,128)} collective-permute-done((f32[4,512,64]{1,2,0:T(8,128)}, f32[4,512,64]{1,2,0:T(8,128)}, u32[]{:S(2)}, u32[]{:S(2)}) %collective-permute-start.6) | collective-permute-done | bytes 524320 | tf_op jit(solution)/shard_map/ppermute | solution.py:22
  422.2 13.4 %collective-permute-start.8 = (f32[4,64,256]{1,2,0:T(8,128)S(1)}, f32[4,64,256]{1,2,0:T(8,128)S(1)}, u32[]{:S(2)}, u32[]{:S(2)}) collective-permute-start(f32[4,64,256]{1,2,0:T(8,128)S(1)} %get-tuple-element.754), channel_id=1, source_target_pairs={{0,8},{8,16},{16,24},{24,0},{1,9},{9,17},{17,25},{25,1},{2,10},{10... | collective-permute-start | bytes 786440 | tf_op jit(solution)/shard_map/ppermute | solution.py:22
  435.6 7.3 collective-permute-done.8
  442.9 18.6 %collective-permute-done.9 = f32[4,64,256]{1,2,0:T(8,128)S(1)} collective-permute-done((f32[4,64,256]{1,2,0:T(8,128)S(1)}, f32[4,64,256]{1,2,0:T(8,128)S(1)}, u32[]{:S(2)}, u32[]{:S(2)}) %collective-permute-start.9) | collective-permute-done | bytes 262176 | tf_op jit(solution)/shard_map/ppermute | solution.py:25
  463.6 16.5 %collective-permute-start.10 = (f32[4,384,64]{1,2,0:T(8,128)}, f32[4,384,64]{1,2,0:T(8,128)S(1)}, u32[]{:S(2)}, u32[]{:S(2)}) collective-permute-start(f32[4,384,64]{1,2,0:T(8,128)} %get-tuple-element.750), channel_id=1, source_target_pairs={{0,1},{1,2},{2,3},{3,4},{4,5},{5,6},{6,7},{7,0},{8,9},{9,10},{10,1... | collective-permute-start | bytes 1179656 | tf_op jit(solution)/shard_map/ppermute | solution.py:22
  481.7 14.0 %collective-permute-done.11 = f32[4,384,64]{1,2,0:T(8,128)} collective-permute-done((f32[4,384,64]{1,2,0:T(8,128)}, f32[4,384,64]{1,2,0:T(8,128)}, u32[]{:S(2)}, u32[]{:S(2)}) %collective-permute-start.11) | collective-permute-done | bytes 393248 | tf_op jit(solution)/shard_map/ppermute | solution.py:25
  498.8 9.6 all-gather.5.cloned.1.call-done
  508.4 6.9 reduce_sum.18
  517.8 204.7 %while.33 = (s32[]{:T(128)}, f32[4,384,384]{2,1,0:T(8,128)}, f32[2,256,256]{2,1,0:T(8,128)}, s32[]{:T(128)}, s32[1,1,5,2]{2,3,1,0:T(2,128)S(1)}, /*index=5*/f32[...) while((s32[]{:T(128)}, f32[4,384,384]{2,1,0:T(8,128)}, ...), condition=%wide.region_6.7_spmd.clone.clone, body=%wide.region_5.6_spmd.clone.clone.sunk | while | flops 6464077824 | bytes 48234916 | solution.py:135
  588.7 11.5 %dynamic_update_slice.17 = f32[4,384,384]{2,1,0:T(8,128)} dynamic-update-slice(f32[4,384,384]{2,1,0:T(8,128)} %get-tuple-element.1071, f32[4,256,256]{2,1,0:T(8,128)S(1)} %maximum_add_fusion.10, s32[]{:T(128)} %constant.71.clone.1..sunk.1, s32[]{:T(128)S(6)} %select_n.385, s32[]{:T(128)S(6)} %select_n.386) | dynamic-update-slice | bytes 2097156 | tf_op jit(solution)/shard_map/while/body/dynamic_update_slice | solution.py:128
  647.2 11.3 %dynamic_update_slice.17 = f32[4,384,384]{2,1,0:T(8,128)} dynamic-update-slice(f32[4,384,384]{2,1,0:T(8,128)} %get-tuple-element.1071, f32[4,256,256]{2,1,0:T(8,128)S(1)} %maximum_add_fusion.10, s32[]{:T(128)} %constant.71.clone.1..sunk.1, s32[]{:T(128)S(6)} %select_n.385, s32[]{:T(128)S(6)} %select_n.386) | dynamic-update-slice | bytes 2097156 | tf_op jit(solution)/shard_map/while/body/dynamic_update_slice | solution.py:128
  705.6 11.5 %dynamic_update_slice.17 = f32[4,384,384]{2,1,0:T(8,128)} dynamic-update-slice(f32[4,384,384]{2,1,0:T(8,128)} %get-tuple-element.1071, f32[4,256,256]{2,1,0:T(8,128)S(1)} %maximum_add_fusion.10, s32[]{:T(128)} %constant.71.clone.1..sunk.1, s32[]{:T(128)S(6)} %select_n.385, s32[]{:T(128)S(6)} %select_n.386) | dynamic-update-slice | bytes 2097156 | tf_op jit(solution)/shard_map/while/body/dynamic_update_slice | solution.py:128
  723.8 118.8 %collective-permute-start.13 = (f32[4,64,384]{2,1,0:T(8,128)S(1)}, f32[4,64,384]{2,1,0:T(8,128)S(1)}, u32[]{:S(2)}, u32[]{:S(2)}) collective-permute-start(f32[4,64,384]{2,1,0:T(8,128)S(1)} %get-tuple-element.747), channel_id=1, source_target_pairs={{8,0},{16,8},{24,16},{0,24},{9,1},{17,9},{25,17},{1,25},{10,2},{18... | collective-permute-start | bytes 1179656 | tf_op jit(solution)/shard_map/ppermute | solution.py:25
  845.6 5.9 collective-permute-done.12
  863.1 12.5 %collective-permute-done.14 = f32[4,512,64]{1,2,0:T(8,128)S(1)} collective-permute-done((f32[4,512,64]{1,2,0:T(8,128)}, f32[4,512,64]{1,2,0:T(8,128)S(1)}, u32[]{:S(2)}, u32[]{:S(2)}) %collective-permute-start.14) | collective-permute-done | bytes 524320 | tf_op jit(solution)/shard_map/ppermute | solution.py:22
  883.1 77.2 %all-gather.7.cloned.1.call-done = f32[64,256,256]{2,1,0:T(8,128)} async-done(((f32[2,256,256]{2,1,0:T(8,128)}), f32[64,256,256]{2,1,0:T(8,128)}) %all-gather.7.cloned.1.call-update) | async-done | bytes 16777232 | tf_op jit(solution)/shard_map/all_gather | solution.py:142
  960.3 6.9 reduce_sum.19
  (357 shorter events, 343.4 us)
Async XLA Ops:
  7.2 501.2 %all-gather.5.cloned.1.call-start = ((), (), s32[]{:S(2)}) async-start(), calls=%async_computation | async-start | bytes 17301504 | tf_op jit(solution)/shard_map/all_gather | solution.py:142
  8.8 40.3 %copy-start.3 = (f32[2,2,256,256]{2,3,1,0:T(8,128)}, f32[2,2,256,256]{2,3,1,0:T(8,128)S(1)}, u32[]{:S(2)}) copy-start(f32[2,2,256,256]{2,3,1,0:T(8,128)S(1)} %copy.21) | copy-start | bytes 3145732
  10.1 16.9 %collective-permute-start = (f32[4,64,256]{1,2,0:T(8,128)}, f32[4,64,256]{1,2,0:T(8,128)S(1)}, u32[]{:S(2)}, u32[]{:S(2)}) collective-permute-start(f32[4,64,256]{1,2,0:T(8,128)} %get-tuple-element.756), channel_id=1, source_target_pairs={{0,8},{8,16},{16,24},{24,0},{1,9},{9,17},{17,25},{25,1},{2,10},{10... | collective-permute-start | bytes 786440 | tf_op jit(solution)/shard_map/ppermute | solution.py:22
  13.0 24.6 %collective-permute-start.1 = (f32[4,64,256]{1,2,0:T(8,128)}, f32[4,64,256]{1,2,0:T(8,128)S(1)}, u32[]{:S(2)}, u32[]{:S(2)}) collective-permute-start(f32[4,64,256]{1,2,0:T(8,128)} %get-tuple-element.757), channel_id=1, source_target_pairs={{8,0},{16,8},{24,16},{0,24},{9,1},{17,9},{25,17},{1,25},{10,2},{18... | collective-permute-start | bytes 786440 | tf_op jit(solution)/shard_map/ppermute | solution.py:25
  37.9 11.2 %collective-permute-start.2 = (f32[4,384,64]{1,2,0:T(8,128)S(1)}, f32[4,384,64]{1,2,0:T(8,128)S(1)}, u32[]{:S(2)}, u32[]{:S(2)}) collective-permute-start(f32[4,384,64]{1,2,0:T(8,128)S(1)} %get-tuple-element.752), channel_id=1, source_target_pairs={{0,1},{1,2},{2,3},{3,4},{4,5},{5,6},{6,7},{7,0},{8,9},{9,10},{10,1... | collective-permute-start | bytes 1179656 | tf_op jit(solution)/shard_map/ppermute | solution.py:22
  38.0 11.1 %collective-permute-start.3 = (f32[4,384,64]{1,2,0:T(8,128)S(1)}, f32[4,384,64]{1,2,0:T(8,128)S(1)}, u32[]{:S(2)}, u32[]{:S(2)}) collective-permute-start(f32[4,384,64]{1,2,0:T(8,128)S(1)} %get-tuple-element.753), channel_id=1, source_target_pairs={{1,0},{2,1},{3,2},{4,3},{5,4},{6,5},{7,6},{0,7},{9,8},{10,9},{11,1... | collective-permute-start | bytes 1179656 | tf_op jit(solution)/shard_map/ppermute | solution.py:25
  123.5 13.5 %copy-start.8 = (f32[2,256,256]{2,1,0:T(8,128)}, f32[2,256,256]{2,1,0:T(8,128)S(1)}, u32[]{:S(2)}) copy-start(f32[2,256,256]{2,1,0:T(8,128)S(1)} %maximum_add_fusion.9) | copy-start | bytes 1572868 | tf_op jit(solution)/shard_map/while
  240.4 13.5 %copy-start.8 = (f32[2,256,256]{2,1,0:T(8,128)}, f32[2,256,256]{2,1,0:T(8,128)S(1)}, u32[]{:S(2)}) copy-start(f32[2,256,256]{2,1,0:T(8,128)S(1)} %maximum_add_fusion.9) | copy-start | bytes 1572868 | tf_op jit(solution)/shard_map/while
  260.3 700.0 %all-gather.7.cloned.1.call-start = ((), (), s32[]{:S(2)}) async-start(), calls=%async_computation.1 | async-start | bytes 17301504 | tf_op jit(solution)/shard_map/all_gather | solution.py:142
  261.5 125.5 %collective-permute-start.4 = (f32[4,64,384]{2,1,0:T(8,128)S(1)}, f32[4,64,384]{2,1,0:T(8,128)}, u32[]{:S(2)}, u32[]{:S(2)}) collective-permute-start(f32[4,64,384]{2,1,0:T(8,128)S(1)} %get-tuple-element.748), channel_id=1, source_target_pairs={{0,8},{8,16},{16,24},{24,0},{1,9},{9,17},{17,25},{25,1},{2,10},{10... | collective-permute-start | bytes 1179656 | tf_op jit(solution)/shard_map/ppermute | solution.py:22
  261.6 129.7 %collective-permute-start.5 = (f32[4,64,384]{2,1,0:T(8,128)S(1)}, f32[4,64,384]{2,1,0:T(8,128)S(1)}, u32[]{:S(2)}, u32[]{:S(2)}) collective-permute-start(f32[4,64,384]{2,1,0:T(8,128)S(1)} %get-tuple-element.749), channel_id=1, source_target_pairs={{8,0},{16,8},{24,16},{0,24},{9,1},{17,9},{25,17},{1,25},{10,2},{18... | collective-permute-start | bytes 1179656 | tf_op jit(solution)/shard_map/ppermute | solution.py:25
  394.1 20.2 %collective-permute-start.6 = (f32[4,512,64]{1,2,0:T(8,128)}, f32[4,512,64]{1,2,0:T(8,128)}, u32[]{:S(2)}, u32[]{:S(2)}) collective-permute-start(f32[4,512,64]{1,2,0:T(8,128)} %get-tuple-element.740), channel_id=1, source_target_pairs={{0,1},{1,2},{2,3},{3,4},{4,5},{5,6},{6,7},{7,0},{8,9},{9,10},{10,1... | collective-permute-start | bytes 1572872 | tf_op jit(solution)/shard_map/ppermute | solution.py:22
  399.9 14.6 %collective-permute-start.7 = (f32[4,512,64]{1,2,0:T(8,128)}, f32[4,512,64]{1,2,0:T(8,128)}, u32[]{:S(2)}, u32[]{:S(2)}) collective-permute-start(f32[4,512,64]{1,2,0:T(8,128)} %get-tuple-element.741), channel_id=1, source_target_pairs={{1,0},{2,1},{3,2},{4,3},{5,4},{6,5},{7,6},{0,7},{9,8},{10,9},{11,1... | collective-permute-start | bytes 1572872 | tf_op jit(solution)/shard_map/ppermute | solution.py:25
  401.2 16.2 %copy-start.2 = (f32[4,384,384]{1,2,0:T(8,128)S(1)}, f32[4,384,384]{1,2,0:T(8,128)}, u32[]{:S(2)}) copy-start(f32[4,384,384]{1,2,0:T(8,128)} %copy.25) | copy-start | bytes 7077892
  422.0 76.8 %copy-start.5 = (f32[4,256,256]{1,2,0:T(8,128)}, f32[4,256,256]{1,2,0:T(8,128)S(1)}, u32[]{:S(2)}) copy-start(f32[4,256,256]{1,2,0:T(8,128)S(1)} %fusion.249) | copy-start | bytes 3145732
  422.2 20.7 %collective-permute-start.8 = (f32[4,64,256]{1,2,0:T(8,128)S(1)}, f32[4,64,256]{1,2,0:T(8,128)S(1)}, u32[]{:S(2)}, u32[]{:S(2)}) collective-permute-start(f32[4,64,256]{1,2,0:T(8,128)S(1)} %get-tuple-element.754), channel_id=1, source_target_pairs={{0,8},{8,16},{16,24},{24,0},{1,9},{9,17},{17,25},{25,1},{2,10},{10... | collective-permute-start | bytes 786440 | tf_op jit(solution)/shard_map/ppermute | solution.py:22
  435.6 25.9 %collective-permute-start.9 = (f32[4,64,256]{1,2,0:T(8,128)S(1)}, f32[4,64,256]{1,2,0:T(8,128)S(1)}, u32[]{:S(2)}, u32[]{:S(2)}) collective-permute-start(f32[4,64,256]{1,2,0:T(8,128)S(1)} %get-tuple-element.755), channel_id=1, source_target_pairs={{8,0},{16,8},{24,16},{0,24},{9,1},{17,9},{25,17},{1,25},{10,2},{18... | collective-permute-start | bytes 786440 | tf_op jit(solution)/shard_map/ppermute | solution.py:25
  463.6 18.1 %collective-permute-start.10 = (f32[4,384,64]{1,2,0:T(8,128)}, f32[4,384,64]{1,2,0:T(8,128)S(1)}, u32[]{:S(2)}, u32[]{:S(2)}) collective-permute-start(f32[4,384,64]{1,2,0:T(8,128)} %get-tuple-element.750), channel_id=1, source_target_pairs={{0,1},{1,2},{2,3},{3,4},{4,5},{5,6},{6,7},{7,0},{8,9},{9,10},{10,1... | collective-permute-start | bytes 1179656 | tf_op jit(solution)/shard_map/ppermute | solution.py:22
  480.1 15.5 %collective-permute-start.11 = (f32[4,384,64]{1,2,0:T(8,128)}, f32[4,384,64]{1,2,0:T(8,128)}, u32[]{:S(2)}, u32[]{:S(2)}) collective-permute-start(f32[4,384,64]{1,2,0:T(8,128)} %get-tuple-element.751), channel_id=1, source_target_pairs={{1,0},{2,1},{3,2},{4,3},{5,4},{6,5},{7,6},{0,7},{9,8},{10,9},{11,1... | collective-permute-start | bytes 1179656 | tf_op jit(solution)/shard_map/ppermute | solution.py:25
  723.7 127.8 %collective-permute-start.12 = (f32[4,64,384]{2,1,0:T(8,128)S(1)}, f32[4,64,384]{2,1,0:T(8,128)S(1)}, u32[]{:S(2)}, u32[]{:S(2)}) collective-permute-start(f32[4,64,384]{2,1,0:T(8,128)S(1)} %get-tuple-element.746), channel_id=1, source_target_pairs={{0,8},{8,16},{16,24},{24,0},{1,9},{9,17},{17,25},{25,1},{2,10},{10... | collective-permute-start | bytes 1179656 | tf_op jit(solution)/shard_map/ppermute | solution.py:22
  723.8 131.7 %collective-permute-start.13 = (f32[4,64,384]{2,1,0:T(8,128)S(1)}, f32[4,64,384]{2,1,0:T(8,128)S(1)}, u32[]{:S(2)}, u32[]{:S(2)}) collective-permute-start(f32[4,64,384]{2,1,0:T(8,128)S(1)} %get-tuple-element.747), channel_id=1, source_target_pairs={{8,0},{16,8},{24,16},{0,24},{9,1},{17,9},{25,17},{1,25},{10,2},{18... | collective-permute-start | bytes 1179656 | tf_op jit(solution)/shard_map/ppermute | solution.py:25
  858.3 17.3 %collective-permute-start.14 = (f32[4,512,64]{1,2,0:T(8,128)}, f32[4,512,64]{1,2,0:T(8,128)S(1)}, u32[]{:S(2)}, u32[]{:S(2)}) collective-permute-start(f32[4,512,64]{1,2,0:T(8,128)} %get-tuple-element.738), channel_id=1, source_target_pairs={{0,1},{1,2},{2,3},{3,4},{4,5},{5,6},{6,7},{7,0},{8,9},{9,10},{10,1... | collective-permute-start | bytes 1572872 | tf_op jit(solution)/shard_map/ppermute | solution.py:22
  861.2 14.3 %collective-permute-start.15 = (f32[4,512,64]{1,2,0:T(8,128)}, f32[4,512,64]{1,2,0:T(8,128)S(1)}, u32[]{:S(2)}, u32[]{:S(2)}) collective-permute-start(f32[4,512,64]{1,2,0:T(8,128)} %get-tuple-element.739), channel_id=1, source_target_pairs={{1,0},{2,1},{3,2},{4,3},{5,4},{6,5},{7,6},{0,7},{9,8},{10,9},{11,1... | collective-permute-start | bytes 1572872 | tf_op jit(solution)/shard_map/ppermute | solution.py:25
  863.1 15.3 %copy-start.1 = (f32[4,384,384]{1,2,0:T(8,128)S(1)}, f32[4,384,384]{1,2,0:T(8,128)}, u32[]{:S(2)}) copy-start(f32[4,384,384]{1,2,0:T(8,128)} %copy.30) | copy-start | bytes 7077892
  (16 other events, 63.4 us)
Sparse Core Ops, SparseCore 0:
  260.4 247.9 all-gather.4
  722.7 237.5 all-gather.6
